TPU v7x, 32 devices: a whole 2x2x4 slice. The times are simulated.
32 devices in a mesh: grp: 2 (over core), gx: 4 (over y, x), gy: 4 (over z).
Axes of the slice: x: 2, y: 2, z: 4, core: 2. Of those that a mesh axis runs over, the one named last changes fastest.
Arguments:
- coarse_density: float32 [512, 512, 512], P('gx', ('grp', 'gy')), may hold values from -3 to 3
- fine_density: float32 [32, 128, 256], P('gx', 'gy', 'grp'), may hold values from -96 to 96
- fine_start: float32 [32, 128, 256], P('gx', 'gy', 'grp'), may hold values from -6 to 6
- anchor: int32 [3], replicated, may hold values from 1 to 447
Outputs:
- coarse_potential: float32 [512, 512, 512], P('gx', ('grp', 'gy'))
- fine_potential: float32 [32, 128, 256], P('gx', 'gy', 'grp')
Inputs may be any that keep to these rules, and one draw needn't show every extreme that they name: Along every dimension d the coarse cells anchor[d] - 1 up to anchor[d] + (fine cells along d) / 4 lie inside the coarse grid.
All inputs are finite; a program needn't handle non-finite values.
Results may differ from a plain program's by a relative error of at most 0.00015.
Values sent between devices are 32-bit elements; how exact they have to be, the bound alone decides.
A program may use at most 128 MiB of HBM per device.

v0:
```python
import functools
import math

import jax
import jax.numpy as jnp
import numpy as np
from jax import lax
from jax.experimental import pallas as pl
from jax.experimental.pallas import tpu as pltpu
from jax.sharding import PartitionSpec as P

RATIO = 4
SWEEPS = 8
EVERY = ("gx", "grp", "gy")
VMEM_LIMIT = 60 * 1024 * 1024

highest = lax.Precision.HIGHEST


def with_halo(block, sides, width):
    for axis, dim in sides:
        count = lax.axis_size(axis)
        forward = [(i, i + 1) for i in range(count - 1)]
        backward = [(target, source) for source, target in forward]
        low = lax.ppermute(
            lax.slice_in_dim(block, block.shape[dim] - width, None, axis=dim), axis, forward
        )
        high_side = lax.ppermute(lax.slice_in_dim(block, 0, width, axis=dim), axis, backward)
        block = jnp.concatenate([low, block, high_side], axis=dim)
    return block


def sine_table(amount):
    indices = np.arange(1, amount + 1, dtype=np.int64)
    product = indices[:, None] * indices[None, :] % (2 * (amount + 1))
    return math.sqrt(2.0 / (amount + 1)) * np.sin(product * (math.pi / (amount + 1)))


def eigen_values(amount):
    return -4.0 * np.square(np.sin(np.arange(1, amount + 1) * (math.pi / (2 * (amount + 1)))))


def parity_order(amount):
    return np.concatenate([np.arange(0, amount, 2), np.arange(1, amount, 2)])


def halves(table):
    top = table.astype(np.float32).astype(jnp.bfloat16)
    rest = (table - top.astype(np.float64)).astype(np.float32).astype(jnp.bfloat16)
    return top, rest


def folded_tables(amount):
    table = sine_table(amount)[: amount // 2]
    even, odd = table[:, 0::2], table[:, 1::2]
    forward, inverse = [], []
    for part in (even, odd):
        top, rest = halves(part)
        forward.append(np.concatenate([top, top, rest], axis=0))
        top, rest = halves(part.T)
        inverse.append(np.concatenate([top, top, rest], axis=0))
    return np.stack(forward), np.stack(inverse)


def decay_table(cols, depth):
    lam_z = eigen_values(depth)[parity_order(depth)]
    size = -(eigen_values(cols)[:, None] + lam_z[None, :])
    return (2.0 / (2.0 + size + np.sqrt(size * (size + 4.0)))).astype(np.float32)


def split(values):
    top = values.astype(jnp.bfloat16)
    return top, (values - top.astype(jnp.float32)).astype(jnp.bfloat16)


def reverse_lanes(values):
    rows, width = values.shape
    tiles = width // 128
    index = 127 - lax.broadcasted_iota(jnp.int32, (rows, 128), 1)
    parts = [
        jnp.take_along_axis(values[:, t * 128 : (t + 1) * 128], index, axis=1)
        for t in reversed(range(tiles))
    ]
    return jnp.concatenate(parts, axis=1)


def dot32(left, right):
    return jnp.dot(left, right, preferred_element_type=jnp.float32)


def triple(values):
    top, rest = split(values)
    return jnp.concatenate([top, rest, top], axis=1)


def cols_transform(sine3, values):
    top, rest = split(values)
    return dot32(sine3, jnp.concatenate([top, rest, top], axis=0))


def forward_kernel(shape, chunk, block, depth_table, sine3, sine, decay, ends, out_w, out_t, w, traces, sems):
    rows, cols, depth = shape
    half = depth // 2
    count = rows // chunk
    step = pl.program_id(0)

    def send(index):
        part = pl.ds(index * chunk, chunk)
        return pltpu.make_async_copy(w.at[part], out_w.at[part], sems.at[index])

    values = block[...].reshape(chunk * cols, depth)
    low = values[:, :half]
    high = reverse_lanes(values[:, half:])
    even = dot32(triple(low + high), depth_table[0])
    odd = dot32(triple(low - high), depth_table[1])
    even = even.reshape(chunk, cols, half)
    odd = odd.reshape(chunk, cols, half)
    rate = decay[...]
    for x in range(chunk):
        here = step * chunk + x
        now = cols_transform(sine3[...], jnp.concatenate([even[x], odd[x]], axis=1))
        if x == 0:
            before = w[jnp.maximum(here - 1, 0)]
            before = jnp.where(step == 0, 0.0, before)
        else:
            before = w[here - 1]
        w[here] = rate * (before - now)

    @pl.when(step > 0)
    def _():
        send(step - 1).start()

    @pl.when(step == count - 1)
    def _():
        send(step).start()
        for tile in range(depth // 128):
            lanes = slice(tile * 128, (tile + 1) * 128)
            rate = decay[:, lanes]
            first = ends[:, 0:1] * jnp.ones((1, 128), jnp.float32)
            second = ends[:, 1:2] * jnp.ones((1, 128), jnp.float32)

            def back(i, value):
                base = pl.multiple_of((rows // 8 - 1 - i) * 8, 8)
                got_first, got_second = [None] * 8, [None] * 8
                for x in reversed(range(8)):
                    value = w[base + x, :, lanes] + rate * value
                    got_first[x] = jnp.sum(value * first, axis=0, keepdims=True)
                    got_second[x] = jnp.sum(value * second, axis=0, keepdims=True)
                traces[pl.ds(3 * cols + base, 8), lanes] = jnp.concatenate(got_first, axis=0)
                traces[pl.ds(3 * cols + rows + base, 8), lanes] = jnp.concatenate(got_second, axis=0)
                return value

            start = lax.fori_loop(0, rows // 8, back, jnp.zeros((cols, 128), jnp.float32))
            for index, plane in enumerate((start, w[rows - 1, :, lanes], rate * start)):
                traces[index * cols : (index + 1) * cols, lanes] = jnp.dot(
                    sine[...], plane, precision=highest, preferred_element_type=jnp.float32
                )
        out_t[...] = traces[...].T
        for index in range(count):
            send(index).wait()


def inverse_kernel(shape, chunk, part, back, depth_table, sine3, sine, decay, ends, out, w, known, carry):
    rows, cols, depth = shape
    half = depth // 2
    count = rows // chunk
    step = pl.program_id(0)

    @pl.when(step == 0)
    def _():
        known[...] = back[...].T
        planes = [
            jnp.dot(
                sine[...],
                known[index * cols : (index + 1) * cols],
                precision=highest,
                preferred_element_type=jnp.float32,
            )
            for index in range(3)
        ]
        carry[0] = planes[0] - decay[...] * planes[2]
        carry[1] = planes[1]

    @pl.when(step < count)
    def _():
        rate = decay[...]
        first = ends[:, 0:1] * jnp.ones((1, depth), jnp.float32)
        second = ends[:, 1:2] * jnp.ones((1, depth), jnp.float32)
        value = carry[0]
        for x in range(chunk):
            here = step * chunk + x
            value = rate * (
                value
                + first * known[pl.ds(3 * cols + here, 1)]
                + second * known[pl.ds(3 * cols + rows + here, 1)]
            )
            w[here] = part[x] + value
        carry[0] = value

    @pl.when(step == count - 1)
    def _():
        w[rows - 1] = w[rows - 1] + decay[...] * carry[1]
        carry[0] = jnp.zeros((cols, depth), jnp.float32)

    @pl.when(step >= count)
    def _():
        base = (2 * count - 1 - step) * chunk
        rate = decay[...]
        value = carry[0]
        planes = [None] * chunk
        for x in reversed(range(chunk)):
            value = w[base + x] + rate * value
            planes[x] = cols_transform(sine3[...], value)
        carry[0] = value
        values = jnp.concatenate(planes, axis=0)
        even = dot32(triple(values[:, :half]), depth_table[0])
        odd = dot32(triple(values[:, half:]), depth_table[1])
        result = jnp.concatenate([even + odd, reverse_lanes(even - odd)], axis=1)
        out[...] = result.reshape(chunk, cols, depth)


def local_tables(shape):
    rows, cols, depth = shape
    forward, inverse = folded_tables(depth)
    sine = sine_table(cols)
    top, rest = halves(sine)
    sine3 = np.concatenate([top, top, rest], axis=1)
    ends = np.stack([sine[:, 0], sine[:, -1]], axis=1).astype(np.float32)
    return forward, inverse, (sine3, sine.astype(np.float32), decay_table(cols, depth), ends)


def full(array):
    return pl.BlockSpec(array.shape, lambda i, rank=array.ndim: (0,) * rank)


def swap_sides(planes):
    inner = planes[1:-1].reshape((-1, 2) + planes.shape[1:])[:, ::-1]
    inner = inner.reshape((-1,) + planes.shape[1:])
    zero = jnp.zeros_like(planes[:1])
    return jnp.concatenate([zero, inner, zero], axis=0)


def coarse_solve(density):
    rows, cols, depth = density.shape
    shape = density.shape
    strips = lax.axis_size("gx")
    bands = lax.axis_size(("grp", "gy"))
    devices = strips * bands
    share = depth // devices
    length_0 = rows * strips
    length_1 = cols * bands
    chunk = 8
    count = rows // chunk
    width = 3 * cols + 2 * rows
    forward, inverse, tables = local_tables(shape)
    params = pltpu.CompilerParams(
        dimension_semantics=("arbitrary",), vmem_limit_bytes=VMEM_LIMIT
    )
    swept, traces = pl.pallas_call(
        functools.partial(forward_kernel, shape, chunk),
        grid=(count,),
        in_specs=[pl.BlockSpec((chunk, cols, depth), lambda i: (i, 0, 0)), full(forward)]
        + [full(table) for table in tables],
        out_specs=[pl.BlockSpec(memory_space=pl.ANY), pl.BlockSpec((depth, width), lambda i: (0, 0))],
        out_shape=[
            jax.ShapeDtypeStruct(shape, jnp.float32),
            jax.ShapeDtypeStruct((depth, width), jnp.float32),
        ],
        scratch_shapes=[
            pltpu.VMEM(shape, jnp.float32),
            pltpu.VMEM((width, depth), jnp.float32),
            pltpu.SemaphoreType.DMA((count,)),
        ],
        compiler_params=params,
        name="local_forward",
    )(density, forward, *tables)

    packed = traces.reshape(devices, share, width)
    packed = lax.all_to_all(packed, EVERY, split_axis=0, concat_axis=0, tiled=True)
    back = middle(packed, rows, cols, strips, bands, depth)
    back = lax.all_to_all(back, EVERY, split_axis=0, concat_axis=0, tiled=True)
    back = back.reshape(depth, width)

    return pl.pallas_call(
        functools.partial(inverse_kernel, shape, chunk),
        grid=(2 * count,),
        in_specs=[
            pl.BlockSpec((chunk, cols, depth), lambda i: (jnp.minimum(i, count - 1), 0, 0)),
            full(back),
            full(inverse),
        ]
        + [full(table) for table in tables],
        out_specs=pl.BlockSpec(
            (chunk, cols, depth), lambda i: (jnp.minimum(2 * count - 1 - i, count - 1), 0, 0)
        ),
        out_shape=jax.ShapeDtypeStruct(shape, jnp.float32),
        scratch_shapes=[
            pltpu.VMEM(shape, jnp.float32),
            pltpu.VMEM((width, depth), jnp.float32),
            pltpu.VMEM((2, cols, depth), jnp.float32),
        ],
        compiler_params=params,
        name="local_inverse",
    )(swept, back, inverse, *tables)


def thirds(values):
    first = values.astype(jnp.bfloat16).astype(jnp.float32)
    rest = values - first
    second = rest.astype(jnp.bfloat16).astype(jnp.float32)
    return first, second, rest - second


def wave_kernel(block, sides_0, sides_1, stack_0, stack_1, source_0, source_1, lam_0, lam_1, lam_z, out_0, out_1):
    length_0 = lam_0.shape[0]
    left = jnp.concatenate([sides_0[...], source_1[0]], axis=0)
    right = jnp.concatenate([source_0[0], sides_1[...]], axis=0)
    a1, a2, a3 = thirds(left)
    b1, b2, b3 = thirds(right)
    left = jnp.concatenate([a1, a1, a2, a1, a2, a3], axis=0)
    right = jnp.concatenate([b1, b2, b1, b3, b2, b1], axis=0).astype(jnp.bfloat16)
    offset = lam_1[...] + lam_z[0]
    count_0, count_1 = sides_0.shape[0], sides_1.shape[0]
    total = jnp.zeros((2 * count_0, lam_1.shape[1]), jnp.float32)
    for start in range(0, length_0, block):
        part = slice(start, start + block)
        wave = dot32(left[:, part].T.astype(jnp.bfloat16), right) / (lam_0[part] + offset)
        top, rest = split(wave)
        total += dot32(stack_0[:, part], top) + dot32(stack_0[:, part], rest)
        dims = (((1,), (1,)), ((), ()))
        other = lax.dot_general(stack_1[...], top, dims, preferred_element_type=jnp.float32)
        other += lax.dot_general(stack_1[...], rest, dims, preferred_element_type=jnp.float32)
        out_1[0, :, part] = other[:count_1] + other[count_1:]
    out_0[0] = total[:count_0] + total[count_0:]


def waves(sides_0, sides_1, source_0, source_1, depth):
    share, count_0, length_1 = source_0.shape
    _, count_1, length_0 = source_1.shape
    lam_z = jnp.asarray(eigen_values(depth)[parity_order(depth)].astype(np.float32))
    lam_z = lax.dynamic_slice(lam_z, (lax.axis_index(EVERY) * share,), (share,))
    lam_z = jnp.broadcast_to(lam_z[:, None, None], (share, 1, 128))[:, :, :1]
    lam_0 = eigen_values(length_0).astype(np.float32)[:, None]
    lam_1 = eigen_values(length_1).astype(np.float32)[None, :]
    stacks = [np.concatenate(halves(table), axis=0) for table in (sides_0, sides_1)]
    sides = [table.astype(np.float32) for table in (sides_0, sides_1)]
    fixed = [*sides, *stacks]
    each = lambda shape: pl.BlockSpec((1,) + shape[1:], lambda i: (i, 0, 0))
    out_shape = [jax.ShapeDtypeStruct(part.shape, jnp.float32) for part in (source_0, source_1)]
    return pl.pallas_call(
        functools.partial(wave_kernel, math.gcd(256, length_0)),
        grid=(share,),
        in_specs=[full(table) for table in fixed]
        + [each(source_0.shape), each(source_1.shape), full(lam_0), full(lam_1), each(lam_z.shape)],
        out_specs=[each(part.shape) for part in out_shape],
        out_shape=out_shape,
        compiler_params=pltpu.CompilerParams(
            dimension_semantics=("arbitrary",), vmem_limit_bytes=VMEM_LIMIT
        ),
        name="waves",
    )(*fixed, source_0, source_1, lam_0, lam_1, lam_z)


def middle(packed, rows, cols, strips, bands, depth):
    devices, share, width = packed.shape
    cut = 2 * cols
    length_0 = rows * strips
    length_1 = cols * bands
    table_0, table_1 = sine_table(length_0), sine_table(length_1)
    full_0 = jnp.asarray(table_0.astype(np.float32))
    full_1 = full_0 if length_1 == length_0 else jnp.asarray(table_1.astype(np.float32))
    planes_0 = packed[:, :, :cut].reshape(strips, bands, share, 2, cols)
    planes_0 = planes_0.transpose(0, 3, 2, 1, 4).reshape(2 * strips, share, length_1)
    scaled = packed[:, :, cut : cut + cols].reshape(strips, bands, share, cols)
    scaled = scaled.transpose(0, 2, 1, 3).reshape(strips, 1, share, length_1)
    scaled = jnp.concatenate([scaled, jnp.zeros_like(scaled)], axis=1).reshape(planes_0.shape)
    planes_1 = packed[:, :, 3 * cols :].reshape(strips, bands, share, 2, rows)
    planes_1 = planes_1.transpose(1, 3, 2, 0, 4).reshape(2 * bands, share, length_0)
    source_0 = jnp.einsum("pkj,jl->kpl", scaled - swap_sides(planes_0), full_1, precision=highest)
    source_1 = jnp.einsum("qkj,jl->kql", -swap_sides(planes_1), full_0, precision=highest)
    sides_0 = table_0.reshape(strips, rows, length_0)[:, [0, rows - 1]].reshape(2 * strips, length_0)
    sides_1 = table_1.reshape(bands, cols, length_1)[:, [0, cols - 1]].reshape(2 * bands, length_1)
    wave_0, wave_1 = waves(sides_0, sides_1, source_0, source_1, depth)
    side_0 = planes_0 + jnp.einsum("kpl,jl->pkj", wave_0, full_1, precision=highest)
    side_1 = planes_1 + jnp.einsum("kql,jl->qkj", wave_1, full_0, precision=highest)
    back_0 = swap_sides(side_0).reshape(strips, 2, share, bands, cols)
    back_0 = back_0.transpose(0, 3, 2, 1, 4).reshape(devices, share, cut)
    own = side_0.reshape(strips, 2, share, bands, cols)[:, 0]
    own = own.transpose(0, 2, 1, 3).reshape(devices, share, cols)
    back_1 = swap_sides(side_1).reshape(bands, 2, share, strips, rows)
    back_1 = back_1.transpose(3, 0, 2, 1, 4).reshape(devices, share, 2 * rows)
    return jnp.concatenate([back_0, own, back_1], axis=2)


def weights(fine_index, cell):
    scaled = 2 * fine_index + 1 + RATIO
    bottom = scaled >> 3
    weight = (scaled & 7).astype(jnp.float32) * 0.125
    return jnp.where(cell == bottom, 1.0 - weight, jnp.where(cell == bottom + 1, weight, 0.0))


def end_weights(total):
    result = []
    for index in (-1, total):
        scaled = 2 * index + 1 + RATIO
        result.append((scaled // (2 * RATIO), (scaled % (2 * RATIO)) / (2.0 * RATIO)))
    return result


class Plan:
    def __init__(self, fine, counts):
        self.fine = fine
        self.counts = counts
        self.totals = tuple(size * count for size, count in zip(fine, counts))
        self.bounds = tuple(total // RATIO + 2 for total in self.totals)
        self.reach = [size // RATIO + 6 for size in fine]
        if counts[2] == 2:
            self.reach[2] -= 2
        self.rows = -(-max(self.reach[1], 2 * self.reach[0]) // 8) * 8
        self.marks = tuple(self.reach[2] * i for i in range(4))

    def start(self, dim, index):
        return index * (self.fine[dim] // RATIO) - 2

    def start_z(self, index):
        first = self.start(2, index)
        last = self.bounds[2] - self.reach[2]
        if isinstance(index, int):
            return min(max(first, 0), last)
        return jnp.clip(first, 0, last)


def iota(shape, dim):
    return lax.broadcasted_iota(jnp.int32, shape, dim)


def exact_dot(left, right):
    return sum(dot32(left, part.astype(jnp.bfloat16)) for part in thirds(right))


def faces_kernel(plan, shape, near, anchor, potential, out, slab, plane, sem):
    rows, cols, depth = shape
    bound_x, bound_y, bound_z = plan.bounds
    reach_x, reach_y, reach_z = plan.reach
    count_x, count_y, count_z = plan.counts
    shift_x = anchor[0] - 1 - lax.axis_index("gx") * rows
    band = lax.axis_index("grp") * count_y + lax.axis_index("gy")
    shift_y = anchor[1] - 1 - band * cols
    base_z = anchor[2] - 1
    from_x = jnp.clip(shift_x, 0, rows - near)
    copy = pltpu.make_async_copy(potential.at[pl.ds(from_x, near)], slab, sem)
    copy.start()

    parts = []
    cell = iota((depth, 128), 0) - base_z
    lane = iota((depth, 128), 1)
    ends_z = end_weights(plan.totals[2])
    edge = jnp.zeros((depth, 128), jnp.float32)
    for e, (bottom, weight) in enumerate(ends_z):
        here = jnp.where(cell == bottom, 1.0 - weight, jnp.where(cell == bottom + 1, weight, 0.0))
        edge = jnp.where((lane - plan.marks[3]) % 2 == e, here, edge)
    edge = jnp.where((lane >= plan.marks[3]) & (lane < plan.marks[3] + 2 * reach_x), edge, 0.0)
    for g in range(count_z):
        want = jnp.full((depth, 128), -1, jnp.int32)
        for i in range(3):
            inside = (lane >= plan.marks[i]) & (lane < plan.marks[i + 1])
            want = jnp.where(inside, lane - plan.marks[i] + plan.start_z(g), want)
        hit = (want >= 0) & (want < bound_z) & (cell == want)
        parts.append(jnp.where(hit, 1.0, edge).astype(jnp.bfloat16))
    select_z = jnp.concatenate(parts, axis=1)

    high = count_y * plan.rows
    cell = iota((high, cols), 1) - shift_y
    row = iota((high, cols), 0)
    want = (row // plan.rows) * (plan.fine[1] // RATIO) - 2 + row % plan.rows
    ok = (want >= 0) & (want < bound_y) & (row % plan.rows < reach_y) & (cell == want)
    select_y = jnp.where(ok, 1.0, 0.0)
    cell = iota((plan.rows, cols), 1) - shift_y
    row = iota((plan.rows, cols), 0)
    edge = jnp.zeros((plan.rows, cols), jnp.float32)
    for e, (bottom, weight) in enumerate(end_weights(plan.totals[1])):
        here = jnp.where(cell == bottom, 1.0 - weight, jnp.where(cell == bottom + 1, weight, 0.0))
        edge = jnp.where((row >= e * reach_x) & (row < (e + 1) * reach_x), here, edge)
    select_y = jnp.concatenate([select_y, edge], axis=0).astype(jnp.bfloat16)

    copy.wait()
    for x in range(near):
        line = sum(dot32(part.astype(jnp.bfloat16), select_z) for part in thirds(slab[x]))
        plane[x] = exact_dot(select_y, line)

    cells = []
    for a in range(bound_x):
        place = shift_x + a - from_x
        ok = (place >= 0) & (place < near)
        got = plane[jnp.clip(place, 0, near - 1)]
        cells.append(jnp.where(ok, got, 0.0))
    ends = []
    for bottom, weight in end_weights(plan.totals[0]):
        ends.append((1.0 - weight) * cells[bottom] + weight * cells[bottom + 1])

    lane = iota((plan.rows, 128), 1)
    row = iota((plan.rows, 128), 0)
    for dx in range(count_x):
        first = plan.start(0, dx)
        for g in range(count_z):
            lanes = slice(g * 128, (g + 1) * 128)
            face_y = jnp.zeros((plan.rows, 128), jnp.float32)
            for t in range(reach_x):
                if 0 <= first + t < bound_x:
                    face_y = jnp.where(row % reach_x == t, cells[first + t][high:, lanes], face_y)
            for dy in range(count_y):
                part = slice(dy * plan.rows, (dy + 1) * plan.rows)
                face_z = jnp.zeros((plan.rows, 128), jnp.float32)
                for t in range(reach_x):
                    if 0 <= first + t < bound_x:
                        face_z = jnp.where(
                            (lane - plan.marks[3]) // 2 == t, cells[first + t][part, lanes], face_z
                        )
                value = jnp.where(
                    lane < plan.marks[1],
                    ends[0][part, lanes],
                    jnp.where(
                        lane < plan.marks[2],
                        ends[1][part, lanes],
                        jnp.where(lane < plan.marks[3], face_y, face_z),
                    ),
                )
                out[(dx * count_z + g) * count_y + dy] = value


def box_faces(plan, potential, anchor):
    shape = potential.shape
    near = min(plan.bounds[0], shape[0])
    devices = math.prod(plan.counts)
    return pl.pallas_call(
        functools.partial(faces_kernel, plan, shape, near),
        in_specs=[pl.BlockSpec(memory_space=pltpu.SMEM), pl.BlockSpec(memory_space=pl.ANY)],
        out_specs=pl.BlockSpec(memory_space=pltpu.VMEM),
        out_shape=jax.ShapeDtypeStruct((devices, plan.rows, 128), jnp.float32),
        scratch_shapes=[
            pltpu.VMEM((near,) + shape[1:], jnp.float32),
            pltpu.VMEM((near, (plan.counts[1] + 1) * plan.rows, plan.counts[2] * 128), jnp.float32),
            pltpu.SemaphoreType.DMA,
        ],
        compiler_params=pltpu.CompilerParams(vmem_limit_bytes=VMEM_LIMIT),
        name="faces",
    )(anchor, potential)


def sweep_kernel(plan, width, faces, own, other, out, source, values):
    rows, cols, depth = (size + 2 * width for size in plan.fine)
    depth = 2 * plan.fine[2]
    reach_x, reach_y, reach_z = plan.reach
    total_x, total_y, total_z = plan.totals
    me_x, me_y, me_z = (lax.axis_index(axis) for axis in ("gx", "gy", "grp"))
    at_x = me_x * plan.fine[0] - width
    at_y = me_y * plan.fine[1] - width
    face = jnp.sum(faces[...], axis=0)

    def dot(left, right):
        return jnp.dot(left, right, precision=highest, preferred_element_type=jnp.float32)

    cell = iota((128, depth), 0)
    fine = iota((128, depth), 1)
    expand = []
    for i in range(3):
        place = cell - plan.marks[i]
        table = weights(fine, place + plan.start_z(me_z))
        expand.append(jnp.where((place >= 0) & (place < reach_z), table, 0.0))
    shape = (cols, plan.rows)
    cell = iota(shape, 1)
    table = weights(iota(shape, 0) + at_y, cell + plan.start(1, me_y))
    inner_y = jnp.where(cell < reach_y, table, 0.0)
    shape = (rows, plan.rows)
    cell = iota(shape, 1)
    inner_x = []
    for e in range(2):
        place = cell - e * reach_x
        table = weights(iota(shape, 0) + at_x, place + plan.start(0, me_x))
        inner_x.append(jnp.where((place >= 0) & (place < reach_x), table, 0.0))
    cell = iota((128, 128), 0) - plan.marks[3]
    fine = iota((128, 128), 1)
    edge_x = []
    for e in range(2):
        table = weights(fine + at_x, (cell >> 1) + plan.start(0, me_x))
        edge_x.append(jnp.where((cell >= 0) & (cell < 2 * reach_x) & ((cell & 1) == e), table, 0.0))

    ghost_x = [dot(inner_y, dot(face, expand[e])) for e in range(2)]
    lines = dot(face, expand[2])
    ghost_y = [dot(inner_x[e], lines) for e in range(2)]
    column = dot(inner_y, face)
    ghost_z = [dot(column, edge_x[e]) for e in range(2)]

    y = iota((cols, depth), 0) + at_y
    z = iota((cols, depth), 1)
    scale = jnp.where((y >= 0) & (y < total_y), 1.0 / 6.0, 0.0)

    def whole(index, x):
        mine, theirs = own[index, x], other[index, x]
        left = jnp.where(me_z == 0, mine, theirs)
        right = jnp.where(me_z == 0, theirs, mine)
        return jnp.concatenate([left, right], axis=1)

    for x in range(rows):
        here = at_x + x
        value = whole(0, x) * (-1.0 / (RATIO * RATIO))
        value += jnp.where(here == 0, ghost_x[0], 0.0) + jnp.where(here == total_x - 1, ghost_x[1], 0.0)
        value += jnp.where(y == 0, ghost_y[0][x : x + 1], 0.0)
        value += jnp.where(y == total_y - 1, ghost_y[1][x : x + 1], 0.0)
        value += jnp.where(z == 0, ghost_z[0][:, x : x + 1], 0.0)
        value += jnp.where(z == total_z - 1, ghost_z[1][:, x : x + 1], 0.0)
        source[x] = value
        values[0, x] = whole(1, x)

    for sweep in range(width):
        now, later = sweep % 2, (sweep + 1) % 2
        margin = sweep + 1

        def step(x, carry):
            here = at_x + x
            value = values[now, x]
            total = values[now, x - 1] + values[now, x + 1]
            total += pltpu.roll(value, 1, 0) + pltpu.roll(value, cols - 1, 0)
            total += jnp.where(z == 0, 0.0, pltpu.roll(value, 1, 1))
            total += jnp.where(z == depth - 1, 0.0, pltpu.roll(value, depth - 1, 1))
            keep = jnp.where((here >= 0) & (here < total_x), 1.0, 0.0)
            values[later, x] = (total + source[x]) * (scale * keep)
            return carry

        lax.fori_loop(margin, rows - margin, step, 0)

    for x in range(plan.fine[0]):
        value = values[width % 2, width + x, width : cols - width]
        half = plan.fine[2]
        out[x] = jnp.where(me_z == 0, value[:, :half], value[:, half:])


def body(coarse_density, fine_density, fine_start, anchor):
    fine = fine_start.shape
    counts = tuple(lax.axis_size(axis) for axis in ("gx", "gy", "grp"))
    plan = Plan(fine, counts)
    width = SWEEPS
    both = jnp.stack([fine_density, fine_start])
    both = with_halo(both, (("gx", 1), ("gy", 2)), width)
    other = lax.ppermute(both, "grp", [(0, 1), (1, 0)])

    potential = coarse_solve(coarse_density)
    faces = box_faces(plan, potential, anchor)
    faces = lax.all_to_all(faces, EVERY, split_axis=0, concat_axis=0, tiled=True)
    padded = (fine[0] + 2 * width, fine[1] + 2 * width, 2 * fine[2])
    values = pl.pallas_call(
        functools.partial(sweep_kernel, plan, width),
        out_shape=jax.ShapeDtypeStruct(fine, jnp.float32),
        in_specs=[pl.BlockSpec(memory_space=pltpu.VMEM)] * 3,
        out_specs=pl.BlockSpec(memory_space=pltpu.VMEM),
        scratch_shapes=[pltpu.VMEM(padded, jnp.float32), pltpu.VMEM((2,) + padded, jnp.float32)],
        compiler_params=pltpu.CompilerParams(vmem_limit_bytes=VMEM_LIMIT),
        name="sweeps",
    )(faces, both, other)
    return (potential, values)


def solution(mesh):
    return jax.shard_map(
        body,
        mesh=mesh,
        in_specs=(P("gx", ("grp", "gy"), None), P("gx", "gy", "grp"), P("gx", "gy", "grp"), P()),
        out_specs=(P("gx", ("grp", "gy"), None), P("gx", "gy", "grp")),
        check_vma=False,
    )
```

profile of v0, /device:TPU:0, one launch (start us, length us, event | category | flops | bytes accessed | tf_op | source)
XLA Modules:
  0.0 212.3 jit_solution(6152504945629846913)
XLA Ops:
  0.6 28.8 %local_forward.1 = (f32[128,64,512]{2,1,0:T(8,128)}, f32[512,448]{1,0:T(8,128)}) custom-call(f32[128,64,512]{2,1,0:T(8,128)} %block.1, bf16[2,768,256]{2,1,0:T(8,128)(2,1)} %constant.54.clone.depth_table, bf16[64,192]{1,0:T(8,128)(2,1)} %constant.55.clone.sine3, f32[64,64]{1,0:T(8,128)} %constant.56.clone.sine, f32[64,512]{1,0:T(8,128)} %constant.57.clone.decay, ...), custom_call_target="tpu_custom_call" | custom-call | tf_op jit(solution)/shard_map/local_forward/pallas_call | solution.py:259
  29.4 7.3 %all-to-all-start = ((f32[32,16,448]{2,1,0:T(8,128)}), f32[32,16,448]{2,1,0:T(8,128)S(1)}, u32[]{:S(2)}, u32[]{:S(2)}) async-start(f32[32,16,448]{2,1,0:T(8,128)} %bitcast.76), calls=%async_computation | async-start | bytes 2097152 | tf_op jit(solution)/shard_map/all_to_all | solution.py:279
  36.8 0.8 dynamic-slice_bitcast_fusion
  37.5 0.7 copy.89.lam_z
  38.2 23.5 %all-to-all-done = f32[32,16,448]{2,1,0:T(8,128)S(1)} async-done(((f32[32,16,448]{2,1,0:T(8,128)}), f32[32,16,448]{2,1,0:T(8,128)S(1)}, u32[]{:S(2)}, u32[]{:S(2)}) %all-to-all-start) | async-done | bytes 917536 | tf_op jit(solution)/shard_map/all_to_all | solution.py:279
  65.2 0.9 copy-done
  66.1 1.9 convolution_bitcast_fusion.1.source_1
  68.0 1.5 convolution_bitcast_fusion.3.source_0
  69.5 20.7 %waves.1 = (f32[16,8,512]{2,1,0:T(8,128)}, f32[16,16,512]{2,1,0:T(8,128)}) custom-call(f32[8,512]{1,0:T(8,128)} %constant.61.clone.sides_0, f32[16,512]{1,0:T(8,128)} %constant.62.clone.sides_1, bf16[16,512]{1,0:T(8,128)(2,1)} %constant.63.clone.stack_0, bf16[32,512]{1,0:T(8,128)(2,1)} %constant.64.clone.stack_1, ...), custom_call_target="tpu_custom_call" | custom-call | tf_op jit(solution)/shard_map/waves/pallas_call | solution.py:350
  90.3 2.1 %fusion = f32[8,16,512]{2,0,1:T(8,128)S(1)} fusion(f32[8,16,512]{2,0,1:T(8,128)S(1)} %reshape.79, f32[16,8,512]{2,1,0:T(8,128)} %get-tuple-element.8, f32[512,512,1]{1,0,2:T(8,128)S(1)} %copy-done), kind=kOutput, calls=%fused_computation.5 | convolution fusion | flops 402718720 | bytes 1835008 | tf_op jit(solution)/shard_map/kpl,jl->pkj/dot_general | solution.py:384
  92.9 0.4 copy.91
  93.8 0.8 copy-done.7
  94.7 1.0 convolution_bitcast_fusion
  96.4 0.4 copy.94
  96.8 0.4 reshape.98
  97.2 1.2 pad_maximum_fusion.1
  98.5 4.6 %all-to-all-start.1 = ((f32[32,16,448]{2,1,0:T(8,128)}), f32[32,16,448]{2,1,0:T(8,128)S(1)}, u32[]{:S(2)}, u32[]{:S(2)}) async-start(f32[32,16,448]{2,1,0:T(8,128)} %pad_maximum_fusion.1), calls=%async_computation.1 | async-start | bytes 2097152 | tf_op jit(solution)/shard_map/all_to_all | solution.py:281
  103.1 3.7 %collective-permute-start = (f32[2,8,32,128]{3,2,1,0:T(8,128)S(1)}, f32[2,8,32,128]{3,2,1,0:T(8,128)S(1)}, u32[]{:S(2)}, u32[]{:S(2)}) collective-permute-start(f32[2,8,32,128]{3,2,1,0:T(8,128)S(1)} %pad_maximum_fusion.4), channel_id=1, source_target_pairs={{0,4},{4,8},{8,12},{1,5},{5,9},{9,13},{2,6},{6,10},{10,14},{3,7},{... | collective-permute-start | bytes 786440 | tf_op jit(solution)/shard_map/ppermute | solution.py:25
  106.8 1.3 collective-permute-start.1
  108.1 9.5 %collective-permute-done = f32[2,8,32,128]{3,2,1,0:T(8,128)S(1)} collective-permute-done((f32[2,8,32,128]{3,2,1,0:T(8,128)S(1)}, f32[2,8,32,128]{3,2,1,0:T(8,128)S(1)}, u32[]{:S(2)}, u32[]{:S(2)}) %collective-permute-start) | collective-permute-done | bytes 262176 | tf_op jit(solution)/shard_map/ppermute | solution.py:25
  117.6 10.8 %collective-permute-done.1 = f32[2,8,32,128]{3,2,1,0:T(8,128)S(1)} collective-permute-done((f32[2,8,32,128]{3,2,1,0:T(8,128)S(1)}, f32[2,8,32,128]{3,2,1,0:T(8,128)S(1)}, u32[]{:S(2)}, u32[]{:S(2)}) %collective-permute-start.1) | collective-permute-done | bytes 262176 | tf_op jit(solution)/shard_map/ppermute | solution.py:28
  128.4 4.2 %collective-permute-start.2 = (f32[2,24,8,128]{3,2,1,0:T(8,128)S(1)}, f32[2,24,8,128]{3,2,1,0:T(8,128)S(1)}, u32[]{:S(2)}, u32[]{:S(2)}) collective-permute-start(f32[2,24,8,128]{3,2,1,0:T(8,128)S(1)} %get-tuple-element.10), channel_id=1, source_target_pairs={{0,1},{1,2},{2,3},{4,5},{5,6},{6,7},{8,9},{9,10},{10,11},{12,13},{... | collective-permute-start | bytes 589832 | tf_op jit(solution)/shard_map/ppermute | solution.py:25
  132.6 1.5 collective-permute-start.3
  134.1 2.3 %collective-permute-done.2 = f32[2,24,8,128]{3,2,1,0:T(8,128)S(1)} collective-permute-done((f32[2,24,8,128]{3,2,1,0:T(8,128)S(1)}, f32[2,24,8,128]{3,2,1,0:T(8,128)S(1)}, u32[]{:S(2)}, u32[]{:S(2)}) %collective-permute-start.2) | collective-permute-done | bytes 196640 | tf_op jit(solution)/shard_map/ppermute | solution.py:25
  136.4 4.1 %collective-permute-done.3 = f32[2,24,8,128]{3,2,1,0:T(8,128)S(1)} collective-permute-done((f32[2,24,8,128]{3,2,1,0:T(8,128)S(1)}, f32[2,24,8,128]{3,2,1,0:T(8,128)S(1)}, u32[]{:S(2)}, u32[]{:S(2)}) %collective-permute-start.3) | collective-permute-done | bytes 196640 | tf_op jit(solution)/shard_map/ppermute | solution.py:28
  140.8 1.0 copy-done.2
  141.8 33.4 %local_inverse.1.potential = f32[128,64,512]{2,1,0:T(8,128)} custom-call(f32[128,64,512]{2,1,0:T(8,128)} %get-tuple-element.6.part, f32[512,448]{1,0:T(8,128)} %bitcast.61, bf16[2,768,256]{2,1,0:T(8,128)(2,1)} %constant.67.clone.depth_table, bf16[64,192]{1,0:T(8,128)(2,1)} %constant.55.clone.sine3, f32[64,64]{1,0:T(8,128)} %constant.56.clone.sine, ...), custom_call_target="tpu_custom_call" | custom-call | tf_op jit(solution)/shard_map/local_inverse/pallas_call | solution.py:284
  175.2 6.8 %faces.1 = f32[32,16,128]{2,1,0:T(8,128)} custom-call(s32[3]{0:T(128)} %anchor.1, f32[128,64,512]{2,1,0:T(8,128)} %local_inverse.1.potential), custom_call_target="tpu_custom_call" | custom-call | tf_op jit(solution)/shard_map/faces/pallas_call | solution.py:535
  182.0 3.7 %all-to-all-start.2 = ((f32[32,16,128]{2,1,0:T(8,128)}), f32[32,16,128]{2,1,0:T(8,128)S(1)}, u32[]{:S(2)}, u32[]{:S(2)}) async-start(f32[32,16,128]{2,1,0:T(8,128)} %faces.1), calls=%async_computation.2 | async-start | bytes 524288 | tf_op jit(solution)/shard_map/all_to_all | solution.py:649
  185.7 10.2 %all-to-all-done.2.faces = f32[32,16,128]{2,1,0:T(8,128)S(1)} async-done(((f32[32,16,128]{2,1,0:T(8,128)}), f32[32,16,128]{2,1,0:T(8,128)S(1)}, u32[]{:S(2)}, u32[]{:S(2)}) %all-to-all-start.2) | async-done | bytes 262176 | tf_op jit(solution)/shard_map/all_to_all | solution.py:649
  195.9 0.7 copy-done.6
  196.6 15.7 %sweeps.1 = f32[8,32,128]{2,1,0:T(8,128)} custom-call(f32[32,16,128]{2,1,0:T(8,128)} %copy-done.6, f32[2,24,48,128]{3,2,1,0:T(8,128)} %copy-done.1, f32[2,24,48,128]{3,2,1,0:T(8,128)} %copy-done.5), custom_call_target="tpu_custom_call" | custom-call | tf_op jit(solution)/shard_map/sweeps/pallas_call | solution.py:651
  (55 shorter events, 5.2 us)
Async XLA Ops:
  29.4 32.3 %all-to-all-start = ((f32[32,16,448]{2,1,0:T(8,128)}), f32[32,16,448]{2,1,0:T(8,128)S(1)}, u32[]{:S(2)}, u32[]{:S(2)}) async-start(f32[32,16,448]{2,1,0:T(8,128)} %bitcast.76), calls=%async_computation | async-start | bytes 2097152 | tf_op jit(solution)/shard_map/all_to_all | solution.py:279
  64.9 1.2 copy-start
  93.6 1.0 copy-start.7
  98.5 4.6 %copy-start.3 = (f32[8,32,128]{2,1,0:T(8,128)S(1)}, f32[8,32,128]{2,1,0:T(8,128)}, u32[]{:S(2)}) copy-start(f32[8,32,128]{2,1,0:T(8,128)} %param.20) | copy-start | bytes 393220
  98.5 4.6 %copy-start.4 = (f32[8,32,128]{2,1,0:T(8,128)S(1)}, f32[8,32,128]{2,1,0:T(8,128)}, u32[]{:S(2)}) copy-start(f32[8,32,128]{2,1,0:T(8,128)} %param.19) | copy-start | bytes 393220
  98.5 42.2 %all-to-all-start.1 = ((f32[32,16,448]{2,1,0:T(8,128)}), f32[32,16,448]{2,1,0:T(8,128)S(1)}, u32[]{:S(2)}, u32[]{:S(2)}) async-start(f32[32,16,448]{2,1,0:T(8,128)} %pad_maximum_fusion.1), calls=%async_computation.1 | async-start | bytes 2097152 | tf_op jit(solution)/shard_map/all_to_all | solution.py:281
  103.1 14.5 %collective-permute-start = (f32[2,8,32,128]{3,2,1,0:T(8,128)S(1)}, f32[2,8,32,128]{3,2,1,0:T(8,128)S(1)}, u32[]{:S(2)}, u32[]{:S(2)}) collective-permute-start(f32[2,8,32,128]{3,2,1,0:T(8,128)S(1)} %pad_maximum_fusion.4), channel_id=1, source_target_pairs={{0,4},{4,8},{8,12},{1,5},{5,9},{9,13},{2,6},{6,10},{10,14},{3,7},{... | collective-permute-start | bytes 786440 | tf_op jit(solution)/shard_map/ppermute | solution.py:25
  106.8 21.6 %collective-permute-start.1 = (f32[2,8,32,128]{3,2,1,0:T(8,128)S(1)}, f32[2,8,32,128]{3,2,1,0:T(8,128)S(1)}, u32[]{:S(2)}, u32[]{:S(2)}) collective-permute-start(f32[2,8,32,128]{3,2,1,0:T(8,128)S(1)} %pad_maximum_fusion.4), channel_id=1, source_target_pairs={{4,0},{8,4},{12,8},{5,1},{9,5},{13,9},{6,2},{10,6},{14,10},{7,3},{... | collective-permute-start | bytes 786440 | tf_op jit(solution)/shard_map/ppermute | solution.py:28
  128.4 8.0 %collective-permute-start.2 = (f32[2,24,8,128]{3,2,1,0:T(8,128)S(1)}, f32[2,24,8,128]{3,2,1,0:T(8,128)S(1)}, u32[]{:S(2)}, u32[]{:S(2)}) collective-permute-start(f32[2,24,8,128]{3,2,1,0:T(8,128)S(1)} %get-tuple-element.10), channel_id=1, source_target_pairs={{0,1},{1,2},{2,3},{4,5},{5,6},{6,7},{8,9},{9,10},{10,11},{12,13},{... | collective-permute-start | bytes 589832 | tf_op jit(solution)/shard_map/ppermute | solution.py:25
  132.6 7.9 %collective-permute-start.3 = (f32[2,24,8,128]{3,2,1,0:T(8,128)S(1)}, f32[2,24,8,128]{3,2,1,0:T(8,128)S(1)}, u32[]{:S(2)}, u32[]{:S(2)}) collective-permute-start(f32[2,24,8,128]{3,2,1,0:T(8,128)S(1)} %get-tuple-element.11), channel_id=1, source_target_pairs={{1,0},{2,1},{3,2},{5,4},{6,5},{7,6},{9,8},{10,9},{11,10},{13,12},{... | collective-permute-start | bytes 589832 | tf_op jit(solution)/shard_map/ppermute | solution.py:28
  140.7 34.5 %copy-start.1 = (f32[2,24,48,128]{3,2,1,0:T(8,128)}, f32[2,24,48,128]{3,2,1,0:T(8,128)S(1)}, u32[]{:S(2)}) copy-start(f32[2,24,48,128]{3,2,1,0:T(8,128)S(1)} %pad_maximum_fusion.own) | copy-start | bytes 3538948
  140.7 45.0 %collective-permute-start.4 = (f32[2,24,48,128]{3,2,1,0:T(8,128)S(1)}, f32[2,24,48,128]{3,2,1,0:T(8,128)S(1)}, u32[]{:S(2)}, u32[]{:S(2)}) collective-permute-start(f32[2,24,48,128]{3,2,1,0:T(8,128)S(1)} %pad_maximum_fusion.own), channel_id=1, source_target_pairs={{0,16},{16,0},{1,17},{17,1},{2,18},{18,2},{3,19},{19,3},{4,20},{20... | collective-permute-start | bytes 3538952 | tf_op jit(solution)/shard_map/ppermute | solution.py:645
  140.8 1.0 copy-start.2
  182.0 13.9 %all-to-all-start.2 = ((f32[32,16,128]{2,1,0:T(8,128)}), f32[32,16,128]{2,1,0:T(8,128)S(1)}, u32[]{:S(2)}, u32[]{:S(2)}) async-start(f32[32,16,128]{2,1,0:T(8,128)} %faces.1), calls=%async_computation.2 | async-start | bytes 524288 | tf_op jit(solution)/shard_map/all_to_all | solution.py:649
  185.7 10.2 %copy-start.5 = (f32[2,24,48,128]{3,2,1,0:T(8,128)}, f32[2,24,48,128]{3,2,1,0:T(8,128)S(1)}, u32[]{:S(2)}) copy-start(f32[2,24,48,128]{3,2,1,0:T(8,128)S(1)} %collective-permute-done.4.other) | copy-start | bytes 3538948
  195.9 0.7 copy-start.6
where the time goes:
time: 214 us; the launch traced here: 212 us
  Pallas kernels  105 us (49%)
  waiting for transfers between devices  60.4 us (28%)
  starting transfers between devices  26.3 us (12%)
  local copies, waits for them, and re-layouts  10.9 us (5%)
  matrix products  6.62 us (3%)
    pallas_call x1, Pallas kernels, coarse_solve(): pl.pallas_call(functools.partial(inverse_kernel, shape, chunk), grid=(2 *...  33.4 us
    pallas_call x1, Pallas kernels, coarse_solve(): pl.pallas_call(functools.partial(forward_kernel, shape, chunk), grid=(cou...  28.8 us
    all_to_all x1, waiting for transfers between devices, coarse_solve(): lax.all_to_all(packed, EVERY, split_axis=0, concat_axis=0, tiled=True)  23.5 us
    pallas_call x1, Pallas kernels, waves(): pl.pallas_call(functools.partial(wave_kernel, math.gcd(256, length_0)), g...  20.7 us
    pallas_call x1, Pallas kernels, body(): pl.pallas_call(functools.partial(sweep_kernel, plan, width), out_shape=ja...  15.7 us
    ppermute x2, waiting for transfers between devices, with_halo(): lax.ppermute(lax.slice_in_dim(block, 0, width, axis=dim), axis, backward)  14.9 us
    ppermute x2, waiting for transfers between devices, with_halo(): lax.ppermute(lax.slice_in_dim(block, block.shape[dim] - width, None, axis...  11.8 us
    all_to_all x1, waiting for transfers between devices, body(): lax.all_to_all(faces, EVERY, split_axis=0, concat_axis=0, tiled=True)  10.2 us
  transfers between devices with their start and end apart: 8, of which 6 were waited for; matrix products, arithmetic and copies ran while one was open for 1% of the time, Pallas kernels for 19%

commit v1 on v0

--- a/solution.py
+++ b/solution.py
@@ -9,6 +9,7 @@
 from jax.experimental.pallas import tpu as pltpu
 from jax.sharding import PartitionSpec as P
 
+
 RATIO = 4
 SWEEPS = 8
 EVERY = ("gx", "grp", "gy")
@@ -17,17 +18,15 @@
 highest = lax.Precision.HIGHEST
 
 
-def with_halo(block, sides, width):
-    for axis, dim in sides:
-        count = lax.axis_size(axis)
-        forward = [(i, i + 1) for i in range(count - 1)]
-        backward = [(target, source) for source, target in forward]
-        low = lax.ppermute(
-            lax.slice_in_dim(block, block.shape[dim] - width, None, axis=dim), axis, forward
-        )
-        high_side = lax.ppermute(lax.slice_in_dim(block, 0, width, axis=dim), axis, backward)
-        block = jnp.concatenate([low, block, high_side], axis=dim)
-    return block
+def with_halo(block, axis, dim, width):
+    count = lax.axis_size(axis)
+    forward = [(i, i + 1) for i in range(count - 1)]
+    backward = [(target, source) for source, target in forward]
+    low = lax.ppermute(
+        lax.slice_in_dim(block, block.shape[dim] - width, None, axis=dim), axis, forward
+    )
+    high = lax.ppermute(lax.slice_in_dim(block, 0, width, axis=dim), axis, backward)
+    return jnp.concatenate([low, block, high], axis=dim)
 
 
 def sine_table(amount):
@@ -98,17 +97,28 @@
     return dot32(sine3, jnp.concatenate([top, rest, top], axis=0))
 
 
-def forward_kernel(shape, chunk, block, depth_table, sine3, sine, decay, ends, out_w, out_t, w, traces, sems):
+def forward_kernel(shape, chunk, block, depth_table, sine3, sine, decay, ends, out_w, *rest):
     rows, cols, depth = shape
     half = depth // 2
     count = rows // chunk
     step = pl.program_id(0)
+    *out_t, w, traces, sems, loads = rest
 
     def send(index):
         part = pl.ds(index * chunk, chunk)
         return pltpu.make_async_copy(w.at[part], out_w.at[part], sems.at[index])
 
-    values = block[...].reshape(chunk * cols, depth)
+    def load(index):
+        part = pl.ds(index * chunk, chunk)
+        return pltpu.make_async_copy(block.at[part], w.at[part], loads.at[index])
+
+    @pl.when(step == 0)
+    def _():
+        for index in range(count):
+            load(index).start()
+
+    load(step).wait()
+    values = w[pl.ds(step * chunk, chunk)].reshape(chunk * cols, depth)
     low = values[:, :half]
     high = reverse_lanes(values[:, half:])
     even = dot32(triple(low + high), depth_table[0])
@@ -146,39 +156,56 @@
                     value = w[base + x, :, lanes] + rate * value
                     got_first[x] = jnp.sum(value * first, axis=0, keepdims=True)
                     got_second[x] = jnp.sum(value * second, axis=0, keepdims=True)
-                traces[pl.ds(3 * cols + base, 8), lanes] = jnp.concatenate(got_first, axis=0)
-                traces[pl.ds(3 * cols + rows + base, 8), lanes] = jnp.concatenate(got_second, axis=0)
+                traces[pl.ds(base, 8), lanes] = jnp.concatenate(got_first, axis=0)
+                traces[pl.ds(rows + base, 8), lanes] = jnp.concatenate(got_second, axis=0)
                 return value
 
             start = lax.fori_loop(0, rows // 8, back, jnp.zeros((cols, 128), jnp.float32))
-            for index, plane in enumerate((start, w[rows - 1, :, lanes], rate * start)):
-                traces[index * cols : (index + 1) * cols, lanes] = jnp.dot(
+            for index, plane in enumerate((start, w[rows - 1, :, lanes])):
+                top = 2 * rows + index * cols
+                traces[top : top + cols, lanes] = jnp.dot(
                     sine[...], plane, precision=highest, preferred_element_type=jnp.float32
                 )
-        out_t[...] = traces[...].T
+        size = depth // len(out_t)
+        for index, target in enumerate(out_t):
+            target[...] = traces[:, index * size : (index + 1) * size].T
         for index in range(count):
             send(index).wait()
 
 
-def inverse_kernel(shape, chunk, part, back, depth_table, sine3, sine, decay, ends, out, w, known, carry):
+def inverse_kernel(shape, chunk, parts, swept, *rest):
     rows, cols, depth = shape
     half = depth // 2
     count = rows // chunk
     step = pl.program_id(0)
+    back, rest = rest[:parts], rest[parts:]
+    depth_table, sine3, sine, decay, ends, out, w, known, carry, sems, loads = rest
+
+    def load(index):
+        part = pl.ds(index * chunk, chunk)
+        return pltpu.make_async_copy(swept.at[part], w.at[part], loads.at[index])
+
+    def send(index):
+        part = pl.ds(index * chunk, chunk)
+        return pltpu.make_async_copy(w.at[part], out.at[part], sems.at[index])
 
     @pl.when(step == 0)
     def _():
-        known[...] = back[...].T
+        for index in range(count):
+            load(index).start()
+        size = depth // parts
+        for index in range(parts):
+            known[:, index * size : (index + 1) * size] = back[index][...].T
         planes = [
             jnp.dot(
                 sine[...],
-                known[index * cols : (index + 1) * cols],
+                known[2 * rows + index * cols : 2 * rows + (index + 1) * cols],
                 precision=highest,
                 preferred_element_type=jnp.float32,
             )
-            for index in range(3)
+            for index in range(2)
         ]
-        carry[0] = planes[0] - decay[...] * planes[2]
+        carry[0] = planes[0]
         carry[1] = planes[1]
 
     @pl.when(step < count)
@@ -187,14 +214,15 @@
         first = ends[:, 0:1] * jnp.ones((1, depth), jnp.float32)
         second = ends[:, 1:2] * jnp.ones((1, depth), jnp.float32)
         value = carry[0]
+        load(step).wait()
         for x in range(chunk):
             here = step * chunk + x
             value = rate * (
                 value
-                + first * known[pl.ds(3 * cols + here, 1)]
-                + second * known[pl.ds(3 * cols + rows + here, 1)]
+                + first * known[pl.ds(here, 1)]
+                + second * known[pl.ds(rows + here, 1)]
             )
-            w[here] = part[x] + value
+            w[here] = w[here] + value
         carry[0] = value
 
     @pl.when(step == count - 1)
@@ -204,7 +232,8 @@
 
     @pl.when(step >= count)
     def _():
-        base = (2 * count - 1 - step) * chunk
+        place = 2 * count - 1 - step
+        base = place * chunk
         rate = decay[...]
         value = carry[0]
         planes = [None] * chunk
@@ -216,11 +245,21 @@
         even = dot32(triple(values[:, :half]), depth_table[0])
         odd = dot32(triple(values[:, half:]), depth_table[1])
         result = jnp.concatenate([even + odd, reverse_lanes(even - odd)], axis=1)
-        out[...] = result.reshape(chunk, cols, depth)
+        w[pl.ds(base, chunk)] = result.reshape(chunk, cols, depth)
+
+        @pl.when(step > count)
+        def _():
+            send(place + 1).start()
+
+        @pl.when(step == 2 * count - 1)
+        def _():
+            send(place).start()
+            for index in range(count):
+                send(index).wait()
 
 
 def local_tables(shape):
-    rows, cols, depth = shape
+    _, cols, depth = shape
     forward, inverse = folded_tables(depth)
     sine = sine_table(cols)
     top, rest = halves(sine)
@@ -233,75 +272,72 @@
     return pl.BlockSpec(array.shape, lambda i, rank=array.ndim: (0,) * rank)
 
 
-def swap_sides(planes):
-    inner = planes[1:-1].reshape((-1, 2) + planes.shape[1:])[:, ::-1]
-    inner = inner.reshape((-1,) + planes.shape[1:])
-    zero = jnp.zeros_like(planes[:1])
-    return jnp.concatenate([zero, inner, zero], axis=0)
-
-
 def coarse_solve(density):
     rows, cols, depth = density.shape
     shape = density.shape
     strips = lax.axis_size("gx")
     bands = lax.axis_size(("grp", "gy"))
     devices = strips * bands
-    share = depth // devices
-    length_0 = rows * strips
-    length_1 = cols * bands
-    chunk = 8
+    parts = 2 if depth % (16 * devices) == 0 else 1
+    share = depth // (devices * parts)
+    chunk = 16
     count = rows // chunk
-    width = 3 * cols + 2 * rows
+    width = 2 * cols + 2 * rows
     forward, inverse, tables = local_tables(shape)
     params = pltpu.CompilerParams(
         dimension_semantics=("arbitrary",), vmem_limit_bytes=VMEM_LIMIT
     )
-    swept, traces = pl.pallas_call(
+    swept, *traces = pl.pallas_call(
         functools.partial(forward_kernel, shape, chunk),
         grid=(count,),
-        in_specs=[pl.BlockSpec((chunk, cols, depth), lambda i: (i, 0, 0)), full(forward)]
+        in_specs=[pl.BlockSpec(memory_space=pl.ANY), full(forward)]
         + [full(table) for table in tables],
-        out_specs=[pl.BlockSpec(memory_space=pl.ANY), pl.BlockSpec((depth, width), lambda i: (0, 0))],
-        out_shape=[
-            jax.ShapeDtypeStruct(shape, jnp.float32),
-            jax.ShapeDtypeStruct((depth, width), jnp.float32),
-        ],
+        out_specs=[pl.BlockSpec(memory_space=pl.ANY)]
+        + [pl.BlockSpec((depth // parts, width), lambda i: (0, 0))] * parts,
+        out_shape=[jax.ShapeDtypeStruct(shape, jnp.float32)]
+        + [jax.ShapeDtypeStruct((depth // parts, width), jnp.float32)] * parts,
         scratch_shapes=[
             pltpu.VMEM(shape, jnp.float32),
             pltpu.VMEM((width, depth), jnp.float32),
             pltpu.SemaphoreType.DMA((count,)),
+            pltpu.SemaphoreType.DMA((count,)),
         ],
         compiler_params=params,
+        cost_estimate=cost(30e9),
         name="local_forward",
     )(density, forward, *tables)
 
-    packed = traces.reshape(devices, share, width)
-    packed = lax.all_to_all(packed, EVERY, split_axis=0, concat_axis=0, tiled=True)
-    back = middle(packed, rows, cols, strips, bands, depth)
-    back = lax.all_to_all(back, EVERY, split_axis=0, concat_axis=0, tiled=True)
-    back = back.reshape(depth, width)
+    back = []
+    for index in range(parts):
+        packed = lax.all_to_all(
+            traces[index].reshape(devices, share, width), EVERY, split_axis=0, concat_axis=0, tiled=True
+        )
+        sides = middle(packed, rows, cols, strips, bands, depth, index * devices * share)
+        sides = lax.all_to_all(sides, EVERY, split_axis=0, concat_axis=0, tiled=True)
+        back.append(sides.reshape(depth // parts, width))
 
     return pl.pallas_call(
-        functools.partial(inverse_kernel, shape, chunk),
+        functools.partial(inverse_kernel, shape, chunk, parts),
         grid=(2 * count,),
         in_specs=[
-            pl.BlockSpec((chunk, cols, depth), lambda i: (jnp.minimum(i, count - 1), 0, 0)),
-            full(back),
+            pl.BlockSpec(memory_space=pl.ANY),
+            *[full(part) for part in back],
             full(inverse),
         ]
         + [full(table) for table in tables],
-        out_specs=pl.BlockSpec(
-            (chunk, cols, depth), lambda i: (jnp.minimum(2 * count - 1 - i, count - 1), 0, 0)
-        ),
+        out_specs=pl.BlockSpec(memory_space=pl.ANY),
         out_shape=jax.ShapeDtypeStruct(shape, jnp.float32),
         scratch_shapes=[
             pltpu.VMEM(shape, jnp.float32),
             pltpu.VMEM((width, depth), jnp.float32),
             pltpu.VMEM((2, cols, depth), jnp.float32),
+            pltpu.SemaphoreType.DMA((count,)),
+            pltpu.SemaphoreType.DMA((count,)),
         ],
         compiler_params=params,
+        cost_estimate=cost(30e9),
         name="local_inverse",
-    )(swept, back, inverse, *tables)
+    )(swept, *back, inverse, *tables)
 
 
 def thirds(values):
@@ -311,85 +347,198 @@
     return first, second, rest - second
 
 
-def wave_kernel(block, sides_0, sides_1, stack_0, stack_1, source_0, source_1, lam_0, lam_1, lam_z, out_0, out_1):
-    length_0 = lam_0.shape[0]
-    left = jnp.concatenate([sides_0[...], source_1[0]], axis=0)
-    right = jnp.concatenate([source_0[0], sides_1[...]], axis=0)
-    a1, a2, a3 = thirds(left)
-    b1, b2, b3 = thirds(right)
-    left = jnp.concatenate([a1, a1, a2, a1, a2, a3], axis=0)
-    right = jnp.concatenate([b1, b2, b1, b3, b2, b1], axis=0).astype(jnp.bfloat16)
-    offset = lam_1[...] + lam_z[0]
-    count_0, count_1 = sides_0.shape[0], sides_1.shape[0]
+def middle_tables(rows, cols, strips, bands, share):
+    count_0, count_1 = 2 * strips, 2 * bands
+    table_0, table_1 = sine_table(rows * strips), sine_table(cols * bands)
+
+    def stacked(table):
+        top, rest = halves(table)
+        return np.concatenate([top, top, rest], axis=0)
+
+    def ends(table, count, size):
+        picked = table.reshape(count, size, -1)[:, [0, size - 1]].reshape(2 * count, -1)
+        return picked.astype(np.float32), np.concatenate(halves(picked), axis=0)
+
+    def shuffle(count, swap):
+        matrix = np.zeros((count * share, count * share), np.float32)
+        for plane in range(count):
+            other = plane if not swap else ((plane - 1) ^ 1) + 1
+            if 0 <= other < count:
+                for k in range(share):
+                    matrix[k * count + plane, other * share + k] = 1.0
+        return matrix
+
+    blocks = np.kron(np.eye(128 // cols), sine_table(cols))
+    gather_0 = shuffle(count_0, False).astype(jnp.bfloat16)
+    gather_1 = -shuffle(count_1, True)
+    scatter_1 = -gather_1.T
+    tables = [stacked(table_0)]
+    if rows * strips != cols * bands:
+        tables.append(stacked(table_1))
+    return (
+        *tables,
+        stacked(blocks),
+        *ends(table_0, strips, rows),
+        *ends(table_1, bands, cols),
+        gather_0,
+        np.ascontiguousarray(gather_0.T),
+        gather_1.astype(jnp.bfloat16),
+        np.ascontiguousarray(scatter_1).astype(jnp.bfloat16),
+        eigen_values(rows * strips).astype(np.float32)[:, None],
+        eigen_values(cols * bands).astype(np.float32)[None, :],
+        np.tile(eigen_values(cols), bands).astype(np.float32)[None, :],
+    )
+
+
+def middle_kernel(
+    sizes, block, packed, lam_own, full_0, *more,
+):
+    full_1, more = (full_0, more) if sizes[0] * sizes[2] == sizes[1] * sizes[3] else (more[0], more[1:])
+    interfaces(sizes, block, packed, lam_own, full_0, full_1, *more)
+
+
+def interfaces(
+    sizes, block, packed, lam_own, full_0, full_1, blocks, sides_0, stack_0, sides_1, stack_1,
+    gather_0, scatter_0, gather_1, scatter_1, lam_0, lam_1, lam_y, out, source_0, source_1, wave_0, wave_1, planes_0, planes_1,
+):
+    rows, cols, strips, bands, share = sizes
+    count_0, count_1 = 2 * strips, 2 * bands
+    step = pl.program_id(0)
+
+    def swapped(plane, count):
+        other = ((plane - 1) ^ 1) + 1
+        return other if 0 <= other < count else None
+
+    def scaled(values):
+        size = -(lam_y[...] + lam_own[...])
+        rate = 2.0 / (2.0 + size + jnp.sqrt(size * (size + 4.0)))
+        rate = jnp.concatenate([rate] * strips, axis=0)
+        result = []
+        for start in range(0, lam_y.shape[1], 128):
+            part = slice(start, start + 128)
+            value = dot32(triple(values[:, part]), blocks[...]) * rate[:, part]
+            result.append(dot32(triple(value), blocks[...]))
+        return jnp.concatenate(result, axis=1)
+
+    def line(values, plane):
+        return values[plane * share : (plane + 1) * share]
+
+    @pl.when(step == 0)
+    def _():
+        for b in range(bands):
+            for e in range(2):
+                lanes = slice(e * rows, (e + 1) * rows)
+                parts = [packed[s * bands + b, :, lanes] for s in range(strips)]
+                plane = 2 * b + e
+                planes_1[plane * share : (plane + 1) * share] = jnp.concatenate(parts, axis=1)
+        for s in range(strips):
+            for e in range(2):
+                lanes = slice(2 * rows + e * cols, 2 * rows + (e + 1) * cols)
+                parts = [packed[s * bands + b, :, lanes] for b in range(bands)]
+                plane = 2 * s + e
+                planes_0[plane * share : (plane + 1) * share] = jnp.concatenate(parts, axis=1)
+        value = planes_0[...]
+        own = scaled(jnp.concatenate([line(value, 2 * s) for s in range(strips)], axis=0))
+        parts = []
+        for plane in range(count_0):
+            part = jnp.zeros_like(line(value, 0))
+            other = swapped(plane, count_0)
+            if other is not None:
+                part = part - line(value, other)
+            if plane % 2 == 0:
+                part = part + line(own, plane // 2)
+            parts.append(part)
+        value = exact_dot(gather_0[...], jnp.concatenate(parts, axis=0))
+        source_0[...] = dot32(triple(value), full_1[...]).reshape(source_0.shape)
+        value = exact_dot(gather_1[...], planes_1[...])
+        source_1[...] = dot32(triple(value), full_0[...]).reshape(source_1.shape)
+
+    left = jnp.concatenate([sides_0[...], source_1[step]], axis=0)
+    right = jnp.concatenate([source_0[step], sides_1[...]], axis=0)
+    a1, a2 = split(left)
+    b1, b2 = split(right)
+    a1, a2 = a1.astype(jnp.float32), a2.astype(jnp.float32)
+    left = jnp.concatenate([a1, a1, a2], axis=0)
+    right = jnp.concatenate([b1.astype(jnp.float32), b2.astype(jnp.float32), b1.astype(jnp.float32)], axis=0)
+    right = right.astype(jnp.bfloat16)
+    offset = lam_1[...] + lam_own[pl.ds(step, 1)]
     total = jnp.zeros((2 * count_0, lam_1.shape[1]), jnp.float32)
-    for start in range(0, length_0, block):
+    dims = (((1,), (1,)), ((), ()))
+    for start in range(0, lam_0.shape[0], block):
         part = slice(start, start + block)
         wave = dot32(left[:, part].T.astype(jnp.bfloat16), right) / (lam_0[part] + offset)
         top, rest = split(wave)
         total += dot32(stack_0[:, part], top) + dot32(stack_0[:, part], rest)
-        dims = (((1,), (1,)), ((), ()))
         other = lax.dot_general(stack_1[...], top, dims, preferred_element_type=jnp.float32)
         other += lax.dot_general(stack_1[...], rest, dims, preferred_element_type=jnp.float32)
-        out_1[0, :, part] = other[:count_1] + other[count_1:]
-    out_0[0] = total[:count_0] + total[count_0:]
-
-
-def waves(sides_0, sides_1, source_0, source_1, depth):
-    share, count_0, length_1 = source_0.shape
-    _, count_1, length_0 = source_1.shape
-    lam_z = jnp.asarray(eigen_values(depth)[parity_order(depth)].astype(np.float32))
-    lam_z = lax.dynamic_slice(lam_z, (lax.axis_index(EVERY) * share,), (share,))
-    lam_z = jnp.broadcast_to(lam_z[:, None, None], (share, 1, 128))[:, :, :1]
-    lam_0 = eigen_values(length_0).astype(np.float32)[:, None]
-    lam_1 = eigen_values(length_1).astype(np.float32)[None, :]
-    stacks = [np.concatenate(halves(table), axis=0) for table in (sides_0, sides_1)]
-    sides = [table.astype(np.float32) for table in (sides_0, sides_1)]
-    fixed = [*sides, *stacks]
-    each = lambda shape: pl.BlockSpec((1,) + shape[1:], lambda i: (i, 0, 0))
-    out_shape = [jax.ShapeDtypeStruct(part.shape, jnp.float32) for part in (source_0, source_1)]
+        wave_1[step, :, part] = other[:count_1] + other[count_1:]
+    wave_0[step] = total[:count_0] + total[count_0:]
+
+    @pl.when(step == share - 1)
+    def _():
+        value = dot32(triple(wave_0[...].reshape(share * count_0, -1)), full_1[...])
+        value = planes_0[...] + exact_dot(scatter_0[...], value)
+        own = scaled(jnp.concatenate([line(value, 2 * s) for s in range(strips)], axis=0))
+        edge_0 = []
+        for plane in range(count_0):
+            part = jnp.zeros_like(line(value, 0))
+            other = swapped(plane, count_0)
+            if other is not None:
+                part = part + line(value, other)
+            if plane % 2 == 0:
+                part = part - line(own, plane // 2)
+            edge_0.append(part)
+        value = dot32(triple(wave_1[...].reshape(share * count_1, -1)), full_0[...])
+        value = exact_dot(scatter_1[...], value)
+        edge_1 = []
+        for plane in range(count_1):
+            part = line(value, plane)
+            other = swapped(plane, count_1)
+            if other is not None:
+                part = part + planes_1[other * share : (other + 1) * share]
+            edge_1.append(part)
+        for s in range(strips):
+            for b in range(bands):
+                parts = [edge_1[2 * b + e][:, s * rows : (s + 1) * rows] for e in range(2)]
+                parts += [edge_0[2 * s + e][:, b * cols : (b + 1) * cols] for e in range(2)]
+                out[s * bands + b] = jnp.concatenate(parts, axis=1)
+
+
+def middle(packed, rows, cols, strips, bands, depth, offset):
+    _, share, _ = packed.shape
+    sizes = (rows, cols, strips, bands, share)
+    lam = jnp.asarray(eigen_values(depth)[parity_order(depth)].astype(np.float32))
+    lam = lax.dynamic_slice(lam, (offset + lax.axis_index(EVERY) * share,), (share,))
+    tables = middle_tables(*sizes)
+    length_0, length_1 = rows * strips, cols * bands
     return pl.pallas_call(
-        functools.partial(wave_kernel, math.gcd(256, length_0)),
+        functools.partial(middle_kernel, sizes, math.gcd(512, length_0)),
         grid=(share,),
-        in_specs=[full(table) for table in fixed]
-        + [each(source_0.shape), each(source_1.shape), full(lam_0), full(lam_1), each(lam_z.shape)],
-        out_specs=[each(part.shape) for part in out_shape],
-        out_shape=out_shape,
+        in_specs=[
+            full(packed),
+            pl.BlockSpec((share, 1), lambda i: (0, 0)),
+        ]
+        + [full(table) for table in tables],
+        out_specs=pl.BlockSpec(packed.shape, lambda i: (0, 0, 0)),
+        out_shape=jax.ShapeDtypeStruct(packed.shape, jnp.float32),
+        scratch_shapes=[
+            pltpu.VMEM((share, 2 * strips, length_1), jnp.float32),
+            pltpu.VMEM((share, 2 * bands, length_0), jnp.float32),
+            pltpu.VMEM((share, 2 * strips, length_1), jnp.float32),
+            pltpu.VMEM((share, 2 * bands, length_0), jnp.float32),
+            pltpu.VMEM((2 * strips * share, length_1), jnp.float32),
+            pltpu.VMEM((2 * bands * share, length_0), jnp.float32),
+        ],
         compiler_params=pltpu.CompilerParams(
             dimension_semantics=("arbitrary",), vmem_limit_bytes=VMEM_LIMIT
         ),
-        name="waves",
-    )(*fixed, source_0, source_1, lam_0, lam_1, lam_z)
-
-
-def middle(packed, rows, cols, strips, bands, depth):
-    devices, share, width = packed.shape
-    cut = 2 * cols
-    length_0 = rows * strips
-    length_1 = cols * bands
-    table_0, table_1 = sine_table(length_0), sine_table(length_1)
-    full_0 = jnp.asarray(table_0.astype(np.float32))
-    full_1 = full_0 if length_1 == length_0 else jnp.asarray(table_1.astype(np.float32))
-    planes_0 = packed[:, :, :cut].reshape(strips, bands, share, 2, cols)
-    planes_0 = planes_0.transpose(0, 3, 2, 1, 4).reshape(2 * strips, share, length_1)
-    scaled = packed[:, :, cut : cut + cols].reshape(strips, bands, share, cols)
-    scaled = scaled.transpose(0, 2, 1, 3).reshape(strips, 1, share, length_1)
-    scaled = jnp.concatenate([scaled, jnp.zeros_like(scaled)], axis=1).reshape(planes_0.shape)
-    planes_1 = packed[:, :, 3 * cols :].reshape(strips, bands, share, 2, rows)
-    planes_1 = planes_1.transpose(1, 3, 2, 0, 4).reshape(2 * bands, share, length_0)
-    source_0 = jnp.einsum("pkj,jl->kpl", scaled - swap_sides(planes_0), full_1, precision=highest)
-    source_1 = jnp.einsum("qkj,jl->kql", -swap_sides(planes_1), full_0, precision=highest)
-    sides_0 = table_0.reshape(strips, rows, length_0)[:, [0, rows - 1]].reshape(2 * strips, length_0)
-    sides_1 = table_1.reshape(bands, cols, length_1)[:, [0, cols - 1]].reshape(2 * bands, length_1)
-    wave_0, wave_1 = waves(sides_0, sides_1, source_0, source_1, depth)
-    side_0 = planes_0 + jnp.einsum("kpl,jl->pkj", wave_0, full_1, precision=highest)
-    side_1 = planes_1 + jnp.einsum("kql,jl->qkj", wave_1, full_0, precision=highest)
-    back_0 = swap_sides(side_0).reshape(strips, 2, share, bands, cols)
-    back_0 = back_0.transpose(0, 3, 2, 1, 4).reshape(devices, share, cut)
-    own = side_0.reshape(strips, 2, share, bands, cols)[:, 0]
-    own = own.transpose(0, 2, 1, 3).reshape(devices, share, cols)
-    back_1 = swap_sides(side_1).reshape(bands, 2, share, strips, rows)
-    back_1 = back_1.transpose(3, 0, 2, 1, 4).reshape(devices, share, 2 * rows)
-    return jnp.concatenate([back_0, own, back_1], axis=2)
+        cost_estimate=cost(20e9),
+        name="interfaces",
+    )(packed, lam.reshape(share, 1), *tables)
+
+
+def cost(flops):
+    return pl.CostEstimate(flops=int(flops), bytes_accessed=1 << 24, transcendentals=0)
 
 
 def weights(fine_index, cell):
@@ -441,7 +590,7 @@
 def faces_kernel(plan, shape, near, anchor, potential, out, slab, plane, sem):
     rows, cols, depth = shape
     bound_x, bound_y, bound_z = plan.bounds
-    reach_x, reach_y, reach_z = plan.reach
+    reach_x, reach_y, _ = plan.reach
     count_x, count_y, count_z = plan.counts
     shift_x = anchor[0] - 1 - lax.axis_index("gx") * rows
     band = lax.axis_index("grp") * count_y + lax.axis_index("gy")
@@ -616,7 +765,7 @@
         now, later = sweep % 2, (sweep + 1) % 2
         margin = sweep + 1
 
-        def step(x, carry):
+        for x in range(margin, rows - margin):
             here = at_x + x
             value = values[now, x]
             total = values[now, x - 1] + values[now, x + 1]
@@ -625,9 +774,6 @@
             total += jnp.where(z == depth - 1, 0.0, pltpu.roll(value, depth - 1, 1))
             keep = jnp.where((here >= 0) & (here < total_x), 1.0, 0.0)
             values[later, x] = (total + source[x]) * (scale * keep)
-            return carry
-
-        lax.fori_loop(margin, rows - margin, step, 0)
 
     for x in range(plan.fine[0]):
         value = values[width % 2, width + x, width : cols - width]
@@ -635,13 +781,14 @@
         out[x] = jnp.where(me_z == 0, value[:, :half], value[:, half:])
 
 
-def body(coarse_density, fine_density, fine_start, anchor):
+def step_of(coarse_density, fine_density, fine_start, anchor):
     fine = fine_start.shape
     counts = tuple(lax.axis_size(axis) for axis in ("gx", "gy", "grp"))
     plan = Plan(fine, counts)
     width = SWEEPS
     both = jnp.stack([fine_density, fine_start])
-    both = with_halo(both, (("gx", 1), ("gy", 2)), width)
+    both = with_halo(both, "gx", 1, width)
+    both = with_halo(both, "gy", 2, width)
     other = lax.ppermute(both, "grp", [(0, 1), (1, 0)])
 
     potential = coarse_solve(coarse_density)
@@ -662,7 +809,7 @@
 
 def solution(mesh):
     return jax.shard_map(
-        body,
+        step_of,
         mesh=mesh,
         in_specs=(P("gx", ("grp", "gy"), None), P("gx", "gy", "grp"), P("gx", "gy", "grp"), P()),
         out_specs=(P("gx", ("grp", "gy"), None), P("gx", "gy", "grp")),

time: 214 us -> 171 us (0.80)
  waiting for transfers between devices: 60.4 us -> 41.3 us
  Pallas kernels: 105 us -> 88.4 us
  starting transfers between devices: 26.3 us -> 36 us
  local copies, waits for them, and re-layouts: 10.9 us -> 3.04 us
  matrix products: 6.62 us -> 0 us
    all_to_all x3 -> x5, waiting for transfers between devices: 33.7 us -> 20.6 us  [the longest x2 10.4 us: coarse_solve(): lax.all_to_all(traces[index].reshape(devices, share, width), EVERY, split...]
    pallas_call x3 -> x4, Pallas kernels: 69.8 us -> 59 us  [the longest x2 27.1 us: middle(): pl.pallas_call(functools.partial(middle_kernel, sizes, math.gcd(512, leng...]
    all_to_all x3 -> x5, starting transfers between devices: 15.6 us -> 26 us  [the longest x2 11.7 us: coarse_solve(): lax.all_to_all(sides, EVERY, split_axis=0, concat_axis=0, tiled=True)]
    dot_general x4 -> x0, matrix products: 6.62 us -> none  [the longest x1 2.12 us: middle(): jnp.einsum('kpl,jl->pkj', wave_0, full_1, precision=highest)]
    pallas_call x1, Pallas kernels: 28.8 us -> 22.6 us  [coarse_solve(): pl.pallas_call(functools.partial(forward_kernel, shape, chunk), grid=(cou...]
    ppermute x2, waiting for transfers between devices: 14.9 us -> 11.7 us  [with_halo(): lax.ppermute(lax.slice_in_dim(block, 0, width, axis=dim), axis, backward)]
    ppermute x2, waiting for transfers between devices: 11.8 us -> 9.03 us  [with_halo(): lax.ppermute(lax.slice_in_dim(block, block.shape[dim] - width, None, axis...]
    slice x12 -> x0, local copies, waits for them, and re-layouts: 2.6 us -> none  [the longest x2 1.44 us: waves(): lam_z = jnp.broadcast_to(lam_z[:, None, None], (share, 1, 128))[:, :, :1]]
  transfers between devices with their start and end apart: 8 -> 10, of which waited for: 6 -> 6; matrix products, arithmetic and copies ran while one was open for 1% -> 1% of each run, Pallas kernels for 19% -> 35%
where the time goes in v1:
time: 171 us; the launch traced here: 170 us
  Pallas kernels  88.4 us (52%)
  waiting for transfers between devices  41.3 us (24%)
  starting transfers between devices  36 us (21%)
  local copies, waits for them, and re-layouts  3.04 us (2%)
    pallas_call x2, Pallas kernels, middle(): pl.pallas_call(functools.partial(middle_kernel, sizes, math.gcd(512, leng...  27.1 us
    pallas_call x1, Pallas kernels, coarse_solve(): pl.pallas_call(functools.partial(inverse_kernel, shape, chunk, parts), gr...  24.7 us
    pallas_call x1, Pallas kernels, coarse_solve(): pl.pallas_call(functools.partial(forward_kernel, shape, chunk), grid=(cou...  22.6 us
    ppermute x2, waiting for transfers between devices, with_halo(): lax.ppermute(lax.slice_in_dim(block, 0, width, axis=dim), axis, backward)  11.7 us
    all_to_all x2, starting transfers between devices, coarse_solve(): lax.all_to_all(sides, EVERY, split_axis=0, concat_axis=0, tiled=True)  11.7 us
    all_to_all x2, starting transfers between devices, coarse_solve(): lax.all_to_all(traces[index].reshape(devices, share, width), EVERY, split...  11.1 us
    all_to_all x2, waiting for transfers between devices, coarse_solve(): lax.all_to_all(traces[index].reshape(devices, share, width), EVERY, split...  10.4 us
    all_to_all x1, waiting for transfers between devices, step_of(): lax.all_to_all(faces, EVERY, split_axis=0, concat_axis=0, tiled=True)  10.2 us
  transfers between devices with their start and end apart: 10, of which 6 were waited for; matrix products, arithmetic and copies ran while one was open for 1% of the time, Pallas kernels for 35%

profile of v1, /device:TPU:0, one launch (start us, length us, event | category | flops | bytes accessed | tf_op | source)
XLA Modules:
  0.0 169.7 jit_solution(1206763796169698415)
XLA Ops:
  0.6 0.0 copy-start.9
  0.6 22.6 %local_forward.1 = (f32[128,64,512]{2,1,0:T(8,128)}, f32[256,384]{1,0:T(8,128)}, f32[256,384]{1,0:T(8,128)}) custom-call(f32[128,64,512]{2,1,0:T(8,128)} %block.1, bf16[2,768,256]{2,1,0:T(8,128)(2,1)} %constant.63.clone.depth_table, bf16[64,192]{1,0:T(8,128)(2,1)} %constant.64.clone.sine3.rest_3_, f32[64,64]{1,0:T(8,128)} %constant.65.clone.sine.rest_4_, ...), custom_call_target="tpu_custom_call" | custom-call | flops 30000001024 | bytes 16777216 | tf_op jit(solution)/shard_map/local_forward/pallas_call | solution.py:290
  23.2 7.3 %all-to-all-start.2 = ((f32[32,8,384]{2,1,0:T(8,128)}), f32[32,8,384]{2,1,0:T(8,128)S(1)}, u32[]{:S(2)}, u32[]{:S(2)}) async-start(f32[32,8,384]{2,1,0:T(8,128)} %bitcast.18), calls=%async_computation.2 | async-start | bytes 786432 | tf_op jit(solution)/shard_map/all_to_all | solution.py:312
  30.6 0.1 dynamic-slice_bitcast_fusion
  30.7 0.7 copy.41.lam_own
  31.3 0.7 copy.40.lam_own
  32.0 10.4 %all-to-all-done.2.packed = f32[32,8,384]{2,1,0:T(8,128)S(1)} async-done(((f32[32,8,384]{2,1,0:T(8,128)}), f32[32,8,384]{2,1,0:T(8,128)S(1)}, u32[]{:S(2)}, u32[]{:S(2)}) %all-to-all-start.2) | async-done | bytes 393248 | tf_op jit(solution)/shard_map/all_to_all | solution.py:312
  42.4 3.8 %all-to-all-start = ((f32[32,8,384]{2,1,0:T(8,128)}), f32[32,8,384]{2,1,0:T(8,128)S(1)}, u32[]{:S(2)}, u32[]{:S(2)}) async-start(f32[32,8,384]{2,1,0:T(8,128)} %bitcast.17), calls=%async_computation | async-start | bytes 786432 | tf_op jit(solution)/shard_map/all_to_all | solution.py:312
  46.3 13.5 %interfaces.3 = f32[32,8,384]{2,1,0:T(8,128)} custom-call(f32[32,8,384]{2,1,0:T(8,128)} %copy-done.6, f32[8,1]{1,0:T(8,128)} %copy.41.lam_own, bf16[1536,512]{1,0:T(8,128)(2,1)} %constant.69.clone.full_0, bf16[384,128]{1,0:T(8,128)(2,1)} %constant.70.clone.more_0_, f32[8,512]{1,0:T(8,128)} %constant.71.clone.more_1_, ...), custom_call_target="tpu_custom_call" | custom-call | flops 20000000000 | bytes 16777216 | tf_op jit(solution)/shard_map/interfaces/pallas_call | solution.py:514
  59.8 5.8 %all-to-all-start.3 = ((f32[32,8,384]{2,1,0:T(8,128)}), f32[32,8,384]{2,1,0:T(8,128)S(1)}, u32[]{:S(2)}, u32[]{:S(2)}) async-start(f32[32,8,384]{2,1,0:T(8,128)} %interfaces.3), calls=%async_computation.3 | async-start | bytes 786432 | tf_op jit(solution)/shard_map/all_to_all | solution.py:316
  65.7 0.0 copy-start.1
  65.7 0.0 copy-start.2
  65.7 13.6 %interfaces.2 = f32[32,8,384]{2,1,0:T(8,128)} custom-call(f32[32,8,384]{2,1,0:T(8,128)} %copy-done.8, f32[8,1]{1,0:T(8,128)} %copy.40.lam_own, bf16[1536,512]{1,0:T(8,128)(2,1)} %constant.69.clone.full_0, bf16[384,128]{1,0:T(8,128)(2,1)} %constant.70.clone.more_0_, f32[8,512]{1,0:T(8,128)} %constant.71.clone.more_1_, ...), custom_call_target="tpu_custom_call" | custom-call | flops 20000000000 | bytes 16777216 | tf_op jit(solution)/shard_map/interfaces/pallas_call | solution.py:514
  79.3 0.0 all-to-all-done.3
  79.3 5.8 %all-to-all-start.1 = ((f32[32,8,384]{2,1,0:T(8,128)}), f32[32,8,384]{2,1,0:T(8,128)S(1)}, u32[]{:S(2)}, u32[]{:S(2)}) async-start(f32[32,8,384]{2,1,0:T(8,128)} %interfaces.2), calls=%async_computation.1 | async-start | bytes 786432 | tf_op jit(solution)/shard_map/all_to_all | solution.py:316
  85.2 3.7 %collective-permute-start = (f32[2,8,32,128]{3,2,1,0:T(8,128)S(1)}, f32[2,8,32,128]{3,2,1,0:T(8,128)S(1)}, u32[]{:S(2)}, u32[]{:S(2)}) collective-permute-start(f32[2,8,32,128]{3,2,1,0:T(8,128)S(1)} %pad_maximum_fusion.1), channel_id=1, source_target_pairs={{0,4},{4,8},{8,12},{1,5},{5,9},{9,13},{2,6},{6,10},{10,14},{3,7},{... | collective-permute-start | bytes 786440 | tf_op jit(solution)/shard_map/ppermute | solution.py:25
  88.9 1.3 collective-permute-start.1
  90.2 6.5 %collective-permute-done = f32[2,8,32,128]{3,2,1,0:T(8,128)S(1)} collective-permute-done((f32[2,8,32,128]{3,2,1,0:T(8,128)S(1)}, f32[2,8,32,128]{3,2,1,0:T(8,128)S(1)}, u32[]{:S(2)}, u32[]{:S(2)}) %collective-permute-start) | collective-permute-done | bytes 262176 | tf_op jit(solution)/shard_map/ppermute | solution.py:25
  96.7 7.5 %collective-permute-done.1 = f32[2,8,32,128]{3,2,1,0:T(8,128)S(1)} collective-permute-done((f32[2,8,32,128]{3,2,1,0:T(8,128)S(1)}, f32[2,8,32,128]{3,2,1,0:T(8,128)S(1)}, u32[]{:S(2)}, u32[]{:S(2)}) %collective-permute-start.1) | collective-permute-done | bytes 262176 | tf_op jit(solution)/shard_map/ppermute | solution.py:28
  104.3 3.5 %collective-permute-start.2 = (f32[2,24,8,128]{3,2,1,0:T(8,128)S(1)}, f32[2,24,8,128]{3,2,1,0:T(8,128)S(1)}, u32[]{:S(2)}, u32[]{:S(2)}) collective-permute-start(f32[2,24,8,128]{3,2,1,0:T(8,128)S(1)} %get-tuple-element.8), channel_id=1, source_target_pairs={{0,1},{1,2},{2,3},{4,5},{5,6},{6,7},{8,9},{9,10},{10,11},{12,13},{... | collective-permute-start | bytes 589832 | tf_op jit(solution)/shard_map/ppermute | solution.py:25
  107.8 1.5 collective-permute-start.3
  109.3 2.5 %collective-permute-done.2 = f32[2,24,8,128]{3,2,1,0:T(8,128)S(1)} collective-permute-done((f32[2,24,8,128]{3,2,1,0:T(8,128)S(1)}, f32[2,24,8,128]{3,2,1,0:T(8,128)S(1)}, u32[]{:S(2)}, u32[]{:S(2)}) %collective-permute-start.2) | collective-permute-done | bytes 196640 | tf_op jit(solution)/shard_map/ppermute | solution.py:25
  111.8 4.1 %collective-permute-done.3 = f32[2,24,8,128]{3,2,1,0:T(8,128)S(1)} collective-permute-done((f32[2,24,8,128]{3,2,1,0:T(8,128)S(1)}, f32[2,24,8,128]{3,2,1,0:T(8,128)S(1)}, u32[]{:S(2)}, u32[]{:S(2)}) %collective-permute-start.3) | collective-permute-done | bytes 196640 | tf_op jit(solution)/shard_map/ppermute | solution.py:28
  115.9 0.1 pad_maximum_fusion.own
  116.0 0.1 collective-permute-start.4
  116.1 0.9 copy-done.7
  117.0 24.7 %local_inverse.1.potential = f32[128,64,512]{2,1,0:T(8,128)} custom-call(f32[128,64,512]{2,1,0:T(8,128)} %get-tuple-element.5.swept, f32[256,384]{1,0:T(8,128)} %bitcast.19, f32[256,384]{1,0:T(8,128)} %bitcast.16, bf16[2,768,256]{2,1,0:T(8,128)(2,1)} %constant.81.clone.rest_2_, bf16[64,192]{1,0:T(8,128)(2,1)} %constant.64.clone.sine3.rest_3_, ...), custom_call_target="tpu_custom_call" | custom-call | flops 30000001024 | bytes 16777216 | tf_op jit(solution)/shard_map/local_inverse/pallas_call | solution.py:319
  141.7 6.8 %faces.1 = f32[32,16,128]{2,1,0:T(8,128)} custom-call(s32[3]{0:T(128)} %anchor.1, f32[128,64,512]{2,1,0:T(8,128)} %local_inverse.1.potential), custom_call_target="tpu_custom_call" | custom-call | tf_op jit(solution)/shard_map/faces/pallas_call | solution.py:684
  148.5 3.1 %all-to-all-start.4 = ((f32[32,16,128]{2,1,0:T(8,128)}), f32[32,16,128]{2,1,0:T(8,128)S(1)}, u32[]{:S(2)}, u32[]{:S(2)}) async-start(f32[32,16,128]{2,1,0:T(8,128)} %faces.1), calls=%async_computation.4 | async-start | bytes 524288 | tf_op jit(solution)/shard_map/all_to_all | solution.py:796
  151.7 10.2 %all-to-all-done.4.faces = f32[32,16,128]{2,1,0:T(8,128)S(1)} async-done(((f32[32,16,128]{2,1,0:T(8,128)}), f32[32,16,128]{2,1,0:T(8,128)S(1)}, u32[]{:S(2)}, u32[]{:S(2)}) %all-to-all-start.4) | async-done | bytes 262176 | tf_op jit(solution)/shard_map/all_to_all | solution.py:796
  161.9 0.7 copy-done.4
  162.6 7.1 %sweeps.1 = f32[8,32,128]{2,1,0:T(8,128)} custom-call(f32[32,16,128]{2,1,0:T(8,128)} %copy-done.4, f32[2,24,48,128]{3,2,1,0:T(8,128)} %copy-done, f32[2,24,48,128]{3,2,1,0:T(8,128)} %copy-done.3), custom_call_target="tpu_custom_call" | custom-call | tf_op jit(solution)/shard_map/sweeps/pallas_call | solution.py:798
  (20 shorter events, 0.1 us)
Async XLA Ops:
  0.6 30.0 %copy-start.9 = (f32[512]{0:T(512)S(1)}, f32[512]{0:T(512)}, u32[]{:S(2)}) copy-start(f32[512]{0:T(512)} %constant.68.clone) | copy-start | bytes 6148
  23.2 19.2 %all-to-all-start.2 = ((f32[32,8,384]{2,1,0:T(8,128)}), f32[32,8,384]{2,1,0:T(8,128)S(1)}, u32[]{:S(2)}, u32[]{:S(2)}) async-start(f32[32,8,384]{2,1,0:T(8,128)} %bitcast.18), calls=%async_computation.2 | async-start | bytes 786432 | tf_op jit(solution)/shard_map/all_to_all | solution.py:312
  42.4 3.8 %copy-start.6 = (f32[32,8,384]{2,1,0:T(8,128)}, f32[32,8,384]{2,1,0:T(8,128)S(1)}, u32[]{:S(2)}) copy-start(f32[32,8,384]{2,1,0:T(8,128)S(1)} %all-to-all-done.2.packed) | copy-start | bytes 1179652
  42.4 17.4 %all-to-all-start = ((f32[32,8,384]{2,1,0:T(8,128)}), f32[32,8,384]{2,1,0:T(8,128)S(1)}, u32[]{:S(2)}, u32[]{:S(2)}) async-start(f32[32,8,384]{2,1,0:T(8,128)} %bitcast.17), calls=%async_computation | async-start | bytes 786432 | tf_op jit(solution)/shard_map/all_to_all | solution.py:312
  59.8 5.9 %copy-start.8 = (f32[32,8,384]{2,1,0:T(8,128)}, f32[32,8,384]{2,1,0:T(8,128)S(1)}, u32[]{:S(2)}) copy-start(f32[32,8,384]{2,1,0:T(8,128)S(1)} %all-to-all-done.packed) | copy-start | bytes 1179652
  59.8 19.5 %all-to-all-start.3 = ((f32[32,8,384]{2,1,0:T(8,128)}), f32[32,8,384]{2,1,0:T(8,128)S(1)}, u32[]{:S(2)}, u32[]{:S(2)}) async-start(f32[32,8,384]{2,1,0:T(8,128)} %interfaces.3), calls=%async_computation.3 | async-start | bytes 786432 | tf_op jit(solution)/shard_map/all_to_all | solution.py:316
  65.7 19.5 %copy-start.1 = (f32[8,32,128]{2,1,0:T(8,128)S(1)}, f32[8,32,128]{2,1,0:T(8,128)}, u32[]{:S(2)}) copy-start(f32[8,32,128]{2,1,0:T(8,128)} %param.40) | copy-start | bytes 393220
  65.7 19.5 %copy-start.2 = (f32[8,32,128]{2,1,0:T(8,128)S(1)}, f32[8,32,128]{2,1,0:T(8,128)}, u32[]{:S(2)}) copy-start(f32[8,32,128]{2,1,0:T(8,128)} %param.39) | copy-start | bytes 393220
  79.3 25.0 %copy-start.5 = (f32[32,8,384]{2,1,0:T(8,128)}, f32[32,8,384]{2,1,0:T(8,128)S(1)}, u32[]{:S(2)}) copy-start(f32[32,8,384]{2,1,0:T(8,128)S(1)} %all-to-all-done.3) | copy-start | bytes 1179652
  79.3 36.8 %all-to-all-start.1 = ((f32[32,8,384]{2,1,0:T(8,128)}), f32[32,8,384]{2,1,0:T(8,128)S(1)}, u32[]{:S(2)}, u32[]{:S(2)}) async-start(f32[32,8,384]{2,1,0:T(8,128)} %interfaces.2), calls=%async_computation.1 | async-start | bytes 786432 | tf_op jit(solution)/shard_map/all_to_all | solution.py:316
  85.2 11.5 %collective-permute-start = (f32[2,8,32,128]{3,2,1,0:T(8,128)S(1)}, f32[2,8,32,128]{3,2,1,0:T(8,128)S(1)}, u32[]{:S(2)}, u32[]{:S(2)}) collective-permute-start(f32[2,8,32,128]{3,2,1,0:T(8,128)S(1)} %pad_maximum_fusion.1), channel_id=1, source_target_pairs={{0,4},{4,8},{8,12},{1,5},{5,9},{9,13},{2,6},{6,10},{10,14},{3,7},{... | collective-permute-start | bytes 786440 | tf_op jit(solution)/shard_map/ppermute | solution.py:25
  88.9 15.4 %collective-permute-start.1 = (f32[2,8,32,128]{3,2,1,0:T(8,128)S(1)}, f32[2,8,32,128]{3,2,1,0:T(8,128)S(1)}, u32[]{:S(2)}, u32[]{:S(2)}) collective-permute-start(f32[2,8,32,128]{3,2,1,0:T(8,128)S(1)} %pad_maximum_fusion.1), channel_id=1, source_target_pairs={{4,0},{8,4},{12,8},{5,1},{9,5},{13,9},{6,2},{10,6},{14,10},{7,3},{... | collective-permute-start | bytes 786440 | tf_op jit(solution)/shard_map/ppermute | solution.py:28
  104.3 7.5 %collective-permute-start.2 = (f32[2,24,8,128]{3,2,1,0:T(8,128)S(1)}, f32[2,24,8,128]{3,2,1,0:T(8,128)S(1)}, u32[]{:S(2)}, u32[]{:S(2)}) collective-permute-start(f32[2,24,8,128]{3,2,1,0:T(8,128)S(1)} %get-tuple-element.8), channel_id=1, source_target_pairs={{0,1},{1,2},{2,3},{4,5},{5,6},{6,7},{8,9},{9,10},{10,11},{12,13},{... | collective-permute-start | bytes 589832 | tf_op jit(solution)/shard_map/ppermute | solution.py:25
  107.8 8.1 %collective-permute-start.3 = (f32[2,24,8,128]{3,2,1,0:T(8,128)S(1)}, f32[2,24,8,128]{3,2,1,0:T(8,128)S(1)}, u32[]{:S(2)}, u32[]{:S(2)}) collective-permute-start(f32[2,24,8,128]{3,2,1,0:T(8,128)S(1)} %get-tuple-element.9), channel_id=1, source_target_pairs={{1,0},{2,1},{3,2},{5,4},{6,5},{7,6},{9,8},{10,9},{11,10},{13,12},{... | collective-permute-start | bytes 589832 | tf_op jit(solution)/shard_map/ppermute | solution.py:28
  116.0 25.7 %copy-start = (f32[2,24,48,128]{3,2,1,0:T(8,128)}, f32[2,24,48,128]{3,2,1,0:T(8,128)S(1)}, u32[]{:S(2)}) copy-start(f32[2,24,48,128]{3,2,1,0:T(8,128)S(1)} %pad_maximum_fusion.own) | copy-start | bytes 3538948
  116.0 35.7 %collective-permute-start.4 = (f32[2,24,48,128]{3,2,1,0:T(8,128)S(1)}, f32[2,24,48,128]{3,2,1,0:T(8,128)S(1)}, u32[]{:S(2)}, u32[]{:S(2)}) collective-permute-start(f32[2,24,48,128]{3,2,1,0:T(8,128)S(1)} %pad_maximum_fusion.own), channel_id=1, source_target_pairs={{0,16},{16,0},{1,17},{17,1},{2,18},{18,2},{3,19},{19,3},{4,20},{20... | collective-permute-start | bytes 3538952 | tf_op jit(solution)/shard_map/ppermute | solution.py:792
  116.1 0.9 copy-start.7
  148.5 13.4 %all-to-all-start.4 = ((f32[32,16,128]{2,1,0:T(8,128)}), f32[32,16,128]{2,1,0:T(8,128)S(1)}, u32[]{:S(2)}, u32[]{:S(2)}) async-start(f32[32,16,128]{2,1,0:T(8,128)} %faces.1), calls=%async_computation.4 | async-start | bytes 524288 | tf_op jit(solution)/shard_map/all_to_all | solution.py:796
  151.7 10.2 %copy-start.3 = (f32[2,24,48,128]{3,2,1,0:T(8,128)}, f32[2,24,48,128]{3,2,1,0:T(8,128)S(1)}, u32[]{:S(2)}) copy-start(f32[2,24,48,128]{3,2,1,0:T(8,128)S(1)} %collective-permute-done.4.other) | copy-start | bytes 3538948
  161.9 0.7 copy-start.4
